TPU v7x, 32 devices: a whole 2x2x4 slice. The times are simulated.
32 devices in a mesh: samp: 4 (over x, core), feat: 8 (over z, y).
Axes of the slice: x: 2, y: 2, z: 4, core: 2. Of those that a mesh axis runs over, the one named last changes fastest.
Arguments:
- design: float32 [4096, 65536], P('samp', 'feat'), may hold values from -0.09375 to 0.09375
- coefficients: float32 [192, 65536], P(None, 'feat'), may hold values from -3 to 3
- response: float32 [192, 4096], P(None, 'samp'), may hold values from -6 to 6
- active_set: int32 [192, 65536], P(None, 'feat'), may hold values 0 or 1
- lambda_path: float32 [192, 16], P('samp'), may hold values from 0.5 to 4
- lambda_index: int32 [192], P('samp'), may hold values from 1 to 15
Outputs:
- margins: float32 [192, 65536], P('samp', 'feat')
- peak_gradient: float32 [192], P('samp')
- violation: float32 [192], P('samp')
- screen_mass: float32 [192], P('samp')
Inputs may be any that keep to these rules, and one draw needn't show every extreme that they name: `active_set`: 1 marks a feature in the response's active set, 0 one outside it. `lambda_index`: the current point on the response's path; the previous point is the one just below it.
All inputs are finite; a program needn't handle non-finite values. No bound on the sum of `active_set` on one device may be relied on, other than what follows from the above.
Results may differ from a plain program's by a relative error of at most 0.000073.
Values sent between devices are 32-bit elements; how exact they have to be, the bound alone decides.
A program may use at most 128 MiB of HBM per device.

v0:
```python
import jax
import jax.numpy as jnp
from jax import lax
from jax.sharding import PartitionSpec as P

NF = 65536


def body(design, coefficients, response, active_set, lambda_path, lambda_index):
    masked = coefficients * active_set.astype(jnp.float32)
    partial_value = lax.dot_general(
        masked,
        design,
        (((1,), (1,)), ((), ())),
        precision=lax.Precision.HIGHEST,
        preferred_element_type=jnp.float32,
    )
    fitted = lax.psum(partial_value, "feat")
    residual = response - fitted
    share_rows = lambda_path.shape[0]
    own_first = lax.axis_index("samp") * share_rows
    gradient = lax.psum_scatter(
        jnp.dot(
            residual, design, precision=lax.Precision.HIGHEST, preferred_element_type=jnp.float32
        ),
        "samp",
        scatter_dimension=0,
        tiled=True,
    )
    own_active = lax.dynamic_slice_in_dim(active_set, own_first, share_rows, 0)
    positions = jnp.arange(lambda_path.shape[1], dtype=jnp.int32)
    picker_now = (positions[None, :] == lambda_index[:, None]).astype(jnp.float32)
    picker_before = (positions[None, :] == lambda_index[:, None] - 1).astype(jnp.float32)
    lambda_new = jnp.sum(lambda_path * picker_now, axis=1)
    lambda_old = jnp.sum(lambda_path * picker_before, axis=1)
    threshold = 2.0 * lambda_new - lambda_old
    magnitude = jnp.abs(gradient)
    margins = magnitude - threshold[:, None]
    local_peak = jnp.max(magnitude, axis=1)
    inactive = 1.0 - own_active.astype(jnp.float32)
    local_violation = (
        jnp.sum(inactive * jnp.maximum(magnitude - lambda_new[:, None], 0.0), axis=1) / NF
    )
    local_mass = jnp.sum(jnp.maximum(margins, 0.0), axis=1) / NF
    peak_gradient = lax.pmax(local_peak, "feat")
    violation, screen_mass = lax.psum((local_violation, local_mass), "feat")
    return (margins, peak_gradient, violation, screen_mass)


def solution(mesh):
    return jax.shard_map(
        body,
        mesh=mesh,
        in_specs=(
            P("samp", "feat"),
            P(None, "feat"),
            P(None, "samp"),
            P(None, "feat"),
            P("samp", None),
            P("samp"),
        ),
        out_specs=(P("samp", "feat"), P("samp"), P("samp"), P("samp")),
        check_vma=False,
    )
```

profile of v0, /device:TPU:0, one launch (start us, length us, event | category | flops | bytes accessed | tf_op | source)
XLA Modules:
  0.0 260.9 jit_solution(6805318242318605775)
XLA Ops:
  7.2 0.0 copy-start
  7.2 0.0 all-reduce.3.cloned.1.call-start
  7.2 39.6 %fusion = f32[192,1024]{1,0:T(8,128)} fusion(f32[1024,8192]{1,0:T(8,128)} %param.6, f32[192,8192]{1,0:T(8,128)} %param.7, s32[192,8192]{1,0:T(8,128)} %param.9), kind=kOutput, calls=%fused_computation | convolution fusion | flops 19330498560 | bytes 46923776 | tf_op jit(solution)/shard_map/dot_general | solution.py:11
  46.8 0.0 all-reduce.3.cloned.1.call-update
  46.8 0.2 reduce-scatter.2.cloned.1.call-start
  47.0 77.7 %all-reduce.3.cloned.1.call-done = f32[192,1024]{1,0:T(8,128)} async-done(((f32[192,1024]{1,0:T(8,128)}), f32[192,1024]{1,0:T(8,128)}) %all-reduce.3.cloned.1.call-update) | async-done | bytes 786448 | tf_op jit(solution)/shard_map/psum | solution.py:18
  124.8 0.0 copy-done
  124.8 27.9 %fusion.3 = f32[192,8192]{1,0:T(8,128)} fusion(f32[1024,8192]{1,0:T(8,128)} %param.6, f32[192,1024]{1,0:T(8,128)S(1)} %copy-done, f32[192,1024]{1,0:T(8,128)} %all-reduce.3.cloned.1.call-done), kind=kOutput, calls=%fused_computation.7 | convolution fusion | flops 19327549440 | bytes 41418752 | tf_op jit(solution)/shard_map/dot_general | solution.py:23
  152.7 0.0 copy-start.2
  152.7 0.0 copy-start.1
  152.7 0.0 reduce-scatter.2.cloned.1.call-update
  152.7 0.6 copy-done.2
  153.3 0.1 copy-done.1
  153.4 57.4 %reduce-scatter.2.cloned.1.call-done = f32[48,8192]{1,0:T(8,128)} async-done(((f32[192,8192]{1,0:T(8,128)}), f32[48,8192]{1,0:T(8,128)}) %reduce-scatter.2.cloned.1.call-update) | async-done | bytes 1572880 | tf_op jit(solution)/shard_map/reduce_scatter | solution.py:22
  210.9 3.7 %multiply_reduce_fusion = (f32[48]{0:T(128)S(1)}, f32[48]{0:T(128)S(1)}, f32[48]{0:T(128)S(1)}, f32[48,8192]{1,0:T(8,128)}) fusion(s32[192,8192]{1,0:T(8,128)} %param.9, s32[]{:T(128)S(6)} %select_n.3, f32[48,8192]{1,0:T(8,128)} %reduce-scatter.2.cloned.1.call-done, f32[48]{0:T(128)S(1)} %get-tuple-element.6, f32[48]{0:T(128)S(1)} %multiply_subtract_fusion), kind=kLoop, calls=%fused_computation.4 | loop fusion | flops 4325232 | bytes 4719556 | tf_op jit(solution)/shard_map/reduce_sum | solution.py:42
  214.6 21.9 %pmax.7 = f32[48]{0:T(128)} all-reduce(f32[48]{0:T(128)S(1)} %get-tuple-element.5), channel_id=1, replica_groups=mesh['samp'=4,'feat'=8] {'feat'}, use_global_device_ids=true, to_apply=%region_5.0 | all-reduce | flops 48 | bytes 384 | tf_op jit(solution)/shard_map/pmax | solution.py:45
  236.5 17.6 %all-reduce = (f32[48]{0:T(128)}, f32[48]{0:T(128)}) all-reduce(f32[48]{0:T(128)S(1)} %get-tuple-element.15, f32[48]{0:T(128)S(1)} %get-tuple-element.14), channel_id=1, replica_groups=mesh['samp'=4,'feat'=8] {'feat'}, use_global_device_ids=true, to_apply=%region_7.0 | all-reduce | flops 96 | bytes 768 | tf_op jit(solution)/shard_map/psum | solution.py:46
  (4 shorter events, 0.0 us)
Async XLA Ops:
  7.2 117.6 %copy-start = (f32[192,1024]{1,0:T(8,128)S(1)}, f32[192,1024]{1,0:T(8,128)}, u32[]{:S(2)}) copy-start(f32[192,1024]{1,0:T(8,128)} %param.8) | copy-start | bytes 2359300
  7.2 117.6 %all-reduce.3.cloned.1.call-start = ((), (), s32[]{:S(2)}) async-start(), calls=%async_computation.1 | async-start | bytes 1572864 | tf_op jit(solution)/shard_map/psum | solution.py:18
  46.8 164.1 %reduce-scatter.2.cloned.1.call-start = ((), (), s32[]{:S(2)}) async-start(), calls=%async_computation.2 | async-start | bytes 7864320 | tf_op jit(solution)/shard_map/reduce_scatter | solution.py:22
  152.7 0.7 copy-start.2
  152.7 0.7 copy-start.1
Sparse Core Ops, SparseCore 0:
  46.9 77.7 all-reduce.2
  152.8 57.9 reduce-scatter.1
where the time goes:
time: 261 us
  waiting for transfers between devices  135 us (52%)
  matrix products  67.5 us (26%)
  blocking collectives  39.5 us (15%)
  between operations  14.1 us (5%)
  other arithmetic  3.78 us (1%)
    psum x1, waiting for transfers between devices, body(): fitted = lax.psum(partial_value, 'feat')  77.7 us
    reduce_scatter x1, waiting for transfers between devices, body(): lax.psum_scatter(jnp.dot(residual, design, precision=lax.Precision.HIGHES...  57.4 us
    dot_general x1, matrix products, body(): lax.dot_general(masked, design, (((1,), (1,)), ((), ())), precision=lax.P...  39.6 us
    dot_general x1, matrix products, body(): jnp.dot(residual, design, precision=lax.Precision.HIGHEST, preferred_elem...  27.9 us
    pmax x1, blocking collectives, body(): peak_gradient = lax.pmax(local_peak, 'feat')  21.9 us
    psum x1, blocking collectives, body(): violation, screen_mass = lax.psum((local_violation, local_mass), 'feat')  17.6 us
  transfers between devices with their start and end apart: 2, of which 2 were waited for; matrix products, arithmetic and copies ran while one was open for 0% of the time, Pallas kernels for 0%

commit v1 on v0

--- a/solution.py
+++ b/solution.py
@@ -4,6 +4,7 @@
 from jax.sharding import PartitionSpec as P
 
 NF = 65536
+fix_page = lambda xs: jnp.sum(lax.all_gather(xs, "feat"), axis=0)
 
 
 def body(design, coefficients, response, active_set, lambda_path, lambda_index):
@@ -15,7 +16,7 @@
         precision=lax.Precision.HIGHEST,
         preferred_element_type=jnp.float32,
     )
-    fitted = lax.psum(partial_value, "feat")
+    fitted = fix_page(partial_value)
     residual = response - fitted
     share_rows = lambda_path.shape[0]
     own_first = lax.axis_index("samp") * share_rows

time: 261 us -> 287 us (1.100)
  waiting for transfers between devices: 135 us -> 158 us
  other arithmetic: 3.78 us -> 7.3 us
    all_gather x0 -> x1, waiting for transfers between devices: none -> 101 us  [fix_page = lambda xs: jnp.sum(lax.all_gather(xs, 'feat'), axis=0)]
    psum x1 -> x0, waiting for transfers between devices: 77.7 us -> none  [body(): fitted = lax.psum(partial_value, 'feat')]
    reduce_sum x0 -> x1, other arithmetic: none -> 3.52 us  [fix_page = lambda xs: jnp.sum(lax.all_gather(xs, 'feat'), axis=0)]
where the time goes in v1:
time: 287 us
  waiting for transfers between devices  158 us (55%)
  matrix products  67.3 us (23%)
  blocking collectives  39.5 us (14%)
  between operations  14.1 us (5%)
  other arithmetic  7.3 us (3%)
    all_gather x1, waiting for transfers between devices, fix_page = lambda xs: jnp.sum(lax.all_gather(xs, 'feat'), axis=0)  101 us
    reduce_scatter x1, waiting for transfers between devices, body(): lax.psum_scatter(jnp.dot(residual, design, precision=lax.Precision.HIGHES...  56.5 us
    dot_general x1, matrix products, body(): lax.dot_general(masked, design, (((1,), (1,)), ((), ())), precision=lax.P...  39.5 us
    dot_general x1, matrix products, body(): jnp.dot(residual, design, precision=lax.Precision.HIGHEST, preferred_elem...  27.8 us
    pmax x1, blocking collectives, body(): peak_gradient = lax.pmax(local_peak, 'feat')  21.9 us
    psum x1, blocking collectives, body(): violation, screen_mass = lax.psum((local_violation, local_mass), 'feat')  17.6 us
  transfers between devices with their start and end apart: 2, of which 2 were waited for; matrix products, arithmetic and copies ran while one was open for 0% of the time, Pallas kernels for 0%

profile of v1, /device:TPU:0, one launch (start us, length us, event | category | flops | bytes accessed | tf_op | source)
XLA Modules:
  0.0 286.9 jit_solution(16531339173735224070)
XLA Ops:
  7.2 0.0 all-gather.3.cloned.1.call-start
  7.2 39.5 %fusion = f32[192,1024]{1,0:T(8,128)} fusion(f32[1024,8192]{1,0:T(8,128)} %param.6, f32[192,8192]{1,0:T(8,128)} %param.7, s32[192,8192]{1,0:T(8,128)} %param.9), kind=kOutput, calls=%fused_computation | convolution fusion | flops 19330498560 | bytes 46923776 | tf_op jit(solution)/shard_map/dot_general | solution.py:12
  46.7 0.0 copy-start
  46.7 0.0 all-gather.3.cloned.1.call-update
  46.7 0.2 reduce-scatter.2.cloned.1.call-start
  47.0 101.3 %all-gather.3.cloned.1.call-done = f32[1536,1024]{1,0:T(8,128)} async-done(((f32[192,1024]{1,0:T(8,128)}), f32[1536,1024]{1,0:T(8,128)}) %all-gather.3.cloned.1.call-update) | async-done | bytes 6291472 | tf_op jit(solution)/shard_map/all_gather | solution.py:7
  148.3 3.5 %reduce_sum.45 = f32[192,1024]{1,0:T(8,128)S(1)} reduce(f32[8,192,1024]{2,1,0:T(8,128)} %bitcast.3, f32[]{:T(128)} %constant.10.clone.1), dimensions={0}, to_apply=%region_0.0 | reduce | flops 1376256 | bytes 7077892 | tf_op jit(solution)/shard_map/reduce_sum | solution.py:7
  151.8 0.0 copy-done
  151.8 27.8 %fusion.3 = f32[192,8192]{1,0:T(8,128)} fusion(f32[1024,8192]{1,0:T(8,128)} %param.6, f32[192,1024]{1,0:T(8,128)S(1)} %copy-done, f32[192,1024]{1,0:T(8,128)S(1)} %reduce_sum.45), kind=kOutput, calls=%fused_computation.7 | convolution fusion | flops 19327549440 | bytes 41418752 | tf_op jit(solution)/shard_map/dot_general | solution.py:24
  179.6 0.0 copy-start.2
  179.6 0.0 copy-start.1
  179.6 0.0 reduce-scatter.2.cloned.1.call-update
  179.6 0.6 copy-done.2
  180.3 0.1 copy-done.1
  180.4 56.5 %reduce-scatter.2.cloned.1.call-done = f32[48,8192]{1,0:T(8,128)} async-done(((f32[192,8192]{1,0:T(8,128)}), f32[48,8192]{1,0:T(8,128)}) %reduce-scatter.2.cloned.1.call-update) | async-done | bytes 1572880 | tf_op jit(solution)/shard_map/reduce_scatter | solution.py:23
  236.8 3.7 %multiply_reduce_fusion = (f32[48]{0:T(128)S(1)}, f32[48]{0:T(128)S(1)}, f32[48]{0:T(128)S(1)}, f32[48,8192]{1,0:T(8,128)}) fusion(s32[192,8192]{1,0:T(8,128)} %param.9, s32[]{:T(128)S(6)} %select_n.3, f32[48,8192]{1,0:T(8,128)} %reduce-scatter.2.cloned.1.call-done, f32[48]{0:T(128)S(1)} %get-tuple-element.6, f32[48]{0:T(128)S(1)} %multiply_subtract_fusion), kind=kLoop, calls=%fused_computation.4 | loop fusion | flops 4325232 | bytes 4719556 | tf_op jit(solution)/shard_map/reduce_sum | solution.py:43
  240.6 21.9 %pmax.7 = f32[48]{0:T(128)} all-reduce(f32[48]{0:T(128)S(1)} %get-tuple-element.5), channel_id=1, replica_groups=mesh['samp'=4,'feat'=8] {'feat'}, use_global_device_ids=true, to_apply=%region_5.0 | all-reduce | flops 48 | bytes 384 | tf_op jit(solution)/shard_map/pmax | solution.py:46
  262.5 17.6 %all-reduce = (f32[48]{0:T(128)}, f32[48]{0:T(128)}) all-reduce(f32[48]{0:T(128)S(1)} %get-tuple-element.15, f32[48]{0:T(128)S(1)} %get-tuple-element.14), channel_id=1, replica_groups=mesh['samp'=4,'feat'=8] {'feat'}, use_global_device_ids=true, to_apply=%region_7.0 | all-reduce | flops 96 | bytes 768 | tf_op jit(solution)/shard_map/psum | solution.py:47
  (4 shorter events, 0.0 us)
Async XLA Ops:
  7.2 141.2 %all-gather.3.cloned.1.call-start = ((), (), s32[]{:S(2)}) async-start(), calls=%async_computation.2 | async-start | bytes 7077888 | tf_op jit(solution)/shard_map/all_gather | solution.py:7
  46.7 105.1 %copy-start = (f32[192,1024]{1,0:T(8,128)S(1)}, f32[192,1024]{1,0:T(8,128)}, u32[]{:S(2)}) copy-start(f32[192,1024]{1,0:T(8,128)} %param.8) | copy-start | bytes 2359300
  46.7 190.1 %reduce-scatter.2.cloned.1.call-start = ((), (), s32[]{:S(2)}) async-start(), calls=%async_computation.1 | async-start | bytes 7864320 | tf_op jit(solution)/shard_map/reduce_scatter | solution.py:23
  179.6 0.7 copy-start.2
  179.6 0.7 copy-start.1
Sparse Core Ops, SparseCore 0:
  46.9 101.4 all-gather.2
  179.8 57.0 reduce-scatter.1
